TPU v7x, 32 devices: a whole 2x2x4 slice. The times are simulated.
32 devices in a mesh: head: 2 (over x), seq: 16 (over z, y, core).
Axes of the slice: x: 2, y: 2, z: 4, core: 2. Of those that a mesh axis runs over, the one named last changes fastest.
Arguments:
- queries: bfloat16 [8192, 4096], P('seq', 'head'), may hold values from -6 to 6
- keys: bfloat16 [8192, 4096], P('seq', 'head'), may hold values from -6 to 6
- values: bfloat16 [8192, 4096], P('seq', 'head'), may hold values from -6 to 6
- out_grad: bfloat16 [8192, 4096], P('seq', 'head'), may hold values from -8 to 8
- inputs: bfloat16 [8192, 2048], P('seq'), may hold values from -100 to 100
- momentum: float32 [2048, 4096], P('seq', 'head'), may hold values from -6 to 6
- level_weight: int32 [18, 32], replicated, may hold values from 1 to 8
Outputs:
- query_grad: bfloat16 [8192, 4096], P('seq', 'head')
- key_grad: bfloat16 [8192, 4096], P('seq', 'head')
- value_grad: bfloat16 [8192, 4096], P('seq', 'head')
- new_momentum: float32 [2048, 4096], P('seq', 'head')
All inputs are finite; a program needn't handle non-finite values.
Results may differ from a plain program's by a relative error of at most 0.0095.
Values may be sent and summed in bfloat16 or wider, within the bound.
A program may use at most 128 MiB of HBM per device.

v0:
```python
import math

import jax
import jax.numpy as jnp
from jax import lax
from jax.sharding import PartitionSpec as P

D_HEAD = 128


clip_norm = 1024.0
momentum_rate = 0.9


def partner(x, axis, apart):
    return lax.ppermute(x, axis, [(i, i ^ 1 << apart) for i in range(lax.axis_size(axis))])


def bit_length(numbers, count):
    total = jnp.zeros_like(numbers)
    for place in range(count):
        total = total + (jnp.right_shift(numbers, place) > 0).astype(jnp.int32)
    return total


def level_table(level_weight, head_size):
    levels = jnp.arange(level_weight.shape[0], dtype=jnp.float32)
    factor = jnp.exp2(-0.5 * levels) / (8.0 * math.sqrt(head_size))
    return level_weight.astype(jnp.float32) * factor[:, None]


def lookup(level, table):
    onehot = (level[..., None] == jnp.arange(table.shape[0], dtype=jnp.int32)).astype(jnp.float32)
    flat = onehot.reshape(-1, table.shape[0])
    picked = jnp.dot(flat, table, precision=lax.Precision.HIGHEST)
    return picked.reshape(level.shape + (table.shape[1],))


def intra_weights(length, table):
    place = jnp.arange(length, dtype=jnp.int32)
    level = bit_length(jnp.bitwise_xor(place[:, None], place[None, :]), table.shape[0])
    picked = lookup(level, table)
    causal = (place[None, :] <= place[:, None])[..., None]
    return jnp.transpose(jnp.where(causal, picked, jnp.float32(0.0)), (2, 0, 1))


def local_grads(query, key_rows, value_rows, grad_rows, weights):
    scores = jnp.einsum("thd,shd->hts", query, key_rows, preferred_element_type=jnp.float32)
    mixed = (weights * scores).astype(jnp.bfloat16)
    value_part = jnp.einsum("hts,thd->shd", mixed, grad_rows, preferred_element_type=jnp.float32)
    before = jnp.einsum("thd,shd->hts", grad_rows, value_rows, preferred_element_type=jnp.float32)
    dmix = (weights * before).astype(jnp.bfloat16)
    query_part = jnp.einsum("hts,shd->thd", dmix, key_rows, preferred_element_type=jnp.float32)
    key_part = jnp.einsum("hts,thd->shd", dmix, query, preferred_element_type=jnp.float32)
    return (query_part, key_part, value_part)


def body(queries, keys, values, out_grad, inputs, momentum, level_weight):
    length = queries.shape[0]
    per_dev = queries.shape[1] // D_HEAD
    width = per_dev * D_HEAD
    table_all = level_table(level_weight, D_HEAD)
    table = lax.dynamic_slice_in_dim(table_all, lax.axis_index("head") * per_dev, per_dev, 1)
    shape = (length, per_dev, D_HEAD)
    query = queries.reshape(shape)
    key_rows = keys.reshape(shape)
    value_rows = values.reshape(shape)
    grad_rows = out_grad.reshape(shape)
    states = jnp.einsum(
        "thd,the->hde", key_rows, value_rows, preferred_element_type=jnp.float32
    ).astype(jnp.bfloat16)
    grads = jnp.einsum("thd,the->hde", query, grad_rows, preferred_element_type=jnp.float32).astype(
        jnp.bfloat16
    )
    rank = lax.axis_index("seq")
    depth = lax.axis_size("seq").bit_length() - 1
    base_level = length.bit_length() - 1
    empty = jnp.zeros((per_dev, D_HEAD, D_HEAD), jnp.float32)
    piece = lax.all_gather(states[None], "seq", axis=0, tiled=True)
    sources = jnp.arange(piece.shape[0], dtype=jnp.int32)
    level = bit_length(jnp.bitwise_xor(sources, rank), table.shape[0]) + base_level
    add_weight = jnp.where((sources < rank)[:, None], lookup(level, table), jnp.float32(0.0))
    state_sum = jnp.einsum(
        "nh,nhde->hde", add_weight, piece.astype(jnp.float32), precision=lax.Precision.HIGHEST
    )
    block = grads.astype(jnp.float32)
    grad_sum = empty
    for bit in range(depth):
        other = partner(block, "seq", bit)
        weight = table[base_level + bit + 1][:, None, None]
        upper = jnp.bitwise_and(jnp.right_shift(rank, bit), 1) == 1
        grad_sum = grad_sum + jnp.where(upper, jnp.float32(0.0), weight * other)
        block = block + other
    carried = state_sum.astype(jnp.bfloat16)
    returned = grad_sum.astype(jnp.bfloat16)
    weights = intra_weights(length, table)
    query_part, key_part, value_part = local_grads(query, key_rows, value_rows, grad_rows, weights)
    query_grad = query_part + jnp.einsum(
        "the,hde->thd", grad_rows, carried, preferred_element_type=jnp.float32
    )
    key_grad = key_part + jnp.einsum(
        "the,hde->thd", value_rows, returned, preferred_element_type=jnp.float32
    )
    value_grad = value_part + jnp.einsum(
        "thd,hde->the", key_rows, returned, preferred_element_type=jnp.float32
    )
    query_grad = query_grad.astype(jnp.bfloat16).reshape(length, width)
    key_grad = key_grad.astype(jnp.bfloat16).reshape(length, width)
    value_grad = value_grad.astype(jnp.bfloat16).reshape(length, width)
    shard = lax.psum_scatter(
        lax.dot_general(
            inputs, value_grad, (((0,), (0,)), ((), ())), preferred_element_type=jnp.float32
        ),
        "seq",
        scatter_dimension=0,
        tiled=True,
    )
    total = lax.psum(jnp.sum(shard * shard), ("head", "seq"))
    factor = jnp.minimum(jnp.float32(1.0), clip_norm / jnp.sqrt(total + 1e-06))
    new_momentum = momentum_rate * momentum + factor * shard
    return (query_grad, key_grad, value_grad, new_momentum)


def solution(mesh):
    placed = (
        P("seq", "head"),
        P("seq", "head"),
        P("seq", "head"),
        P("seq", "head"),
        P("seq", None),
        P("seq", "head"),
        P(),
    )
    return jax.shard_map(
        body,
        mesh=mesh,
        in_specs=placed,
        out_specs=(P("seq", "head"), P("seq", "head"), P("seq", "head"), P("seq", "head")),
        check_vma=False,
    )
```

profile of v0, /device:TPU:0, one launch (start us, length us, event | category | flops | bytes accessed | tf_op | source)
XLA Modules:
  0.0 403.6 jit_solution(13690692763841086824)
XLA Ops:
  7.2 0.0 copy-start
  7.2 0.0 all-gather.3.cloned.1.call-start
  7.2 1.5 copy-done
  8.8 3.3 fusion.41
  12.1 0.0 all-gather.3.cloned.1.call-update
  12.1 0.0 reduce-scatter.2.cloned.1.call-start
  12.1 3.9 copy.115
  16.1 3.0 fusion.49
  19.1 0.6 collective-permute-start
  19.6 0.1 iota_compare_fusion.2
  19.7 2.3 collective-permute-done
  22.0 1.4 add.322
  23.5 2.9 collective-permute-start.1
  26.4 0.1 fusion.55
  26.5 4.0 fusion.29
  30.4 26.7 %collective-permute-done.1 = f32[16,128,128]{2,1,0:T(8,128)S(1)} collective-permute-done((f32[16,128,128]{2,1,0:T(8,128)S(1)}, f32[16,128,128]{2,1,0:T(8,128)S(1)}, u32[]{:S(2)}, u32[]{:S(2)}) %collective-permute-start.1) | collective-permute-done | bytes 1048608 | tf_op jit(solution)/shard_map/ppermute | solution.py:16
  57.1 0.1 add.324
  57.2 1.6 collective-permute-start.2
  58.9 2.4 convert_add_fusion
  61.2 8.1 %fusion.20 = f32[16,512,512]{2,1,0:T(8,128)} fusion(bf16[512,2048]{1,0:T(8,128)(2,1)S(1)} %copy-done.3, bf16[512,2048]{1,0:T(8,128)(2,1)S(1)} %copy-done), kind=kOutput, calls=%fused_computation.25 | convolution fusion | flops 1073741824 | bytes 20971520 | tf_op jit(solution)/shard_map/thd,shd->hts/dot_general | solution.py:48
  69.3 37.4 %collective-permute-done.2 = f32[16,128,128]{2,1,0:T(8,128)S(1)} collective-permute-done((f32[16,128,128]{2,1,0:T(8,128)S(1)}, f32[16,128,128]{2,1,0:T(8,128)S(1)}, u32[]{:S(2)}, u32[]{:S(2)}) %collective-permute-start.2) | collective-permute-done | bytes 1048608 | tf_op jit(solution)/shard_map/ppermute | solution.py:16
  106.8 0.1 add.326
  106.9 0.8 copy-done.7
  107.8 1.0 collective-permute-start.3
  108.8 33.6 %fusion.1 = (bf16[16,512,512]{2,0,1:T(8,128)(2,1)}, bf16[16,512,512]{2,0,1:T(8,128)(2,1)}) fusion(f32[16,512,512]{2,1,0:T(8,128)} %fusion.20, pred[512,512]{1,0:T(8,128)(4,1)S(1)} %iota_compare_fusion.2, f32[16,512,512]{2,1,0:T(8,128)S(1)} %fusion.29, s32[512,512]{1,0:T(8,128)S(1)} %convert_add_fusion, f32[18,16]{1,0:T(8,128)S(1)} %fusion.55), kind=kOutput, calls=%fused_computation.3 | convolution fusion | flops 931659776 | bytes 51643520 | tf_op jit(solution)/shard_map/dot_general | solution.py:35
  142.5 13.2 %fusion.6 = f32[16,512,128]{1,2,0:T(8,128)S(1)} fusion(bf16[512,16,128]{0,2,1:T(8,128)(2,1)} %bitcast.117, bf16[16,512,512]{2,0,1:T(8,128)(2,1)} %get-tuple-element.20), kind=kOutput, calls=%fused_computation.10 | convolution fusion | flops 1073741824 | bytes 14680064 | tf_op jit(solution)/shard_map/hts,thd->shd/dot_general | solution.py:50
  155.7 0.4 collective-permute-done.3
  156.2 2.1 add_convert_fusion
  158.3 0.9 fusion.12
  159.2 1.3 copy-done.4
  160.5 8.4 %convolution_bitcast_fusion = f32[2048,2048]{0,1:T(8,128)} fusion(bf16[512,2048]{0,1:T(8,128)(2,1)S(1)} %bitcast.121, bf16[512,2048]{1,0:T(8,128)(2,1)S(1)} %copy-done.11), kind=kOutput, calls=%fused_computation.7 | convolution fusion | flops 4294967296 | bytes 20971520 | tf_op jit(solution)/shard_map/dot_general | solution.py:111
  168.8 0.0 reduce-scatter.2.cloned.1.call-update
  168.9 2.5 copy.104
  171.4 0.2 fusion.52
  171.6 0.1 copy.110
  171.7 16.9 %fusion.8 = f32[16,512,128]{1,2,0:T(8,128)} fusion(bf16[16,512,512]{2,0,1:T(8,128)(2,1)} %get-tuple-element.21, bf16[512,2048]{1,0:T(8,128)(2,1)} %param.7), kind=kOutput, calls=%fused_computation.12 | convolution fusion | flops 1073741824 | bytes 14680064 | tf_op jit(solution)/shard_map/hts,thd->shd/dot_general | solution.py:54
  188.6 4.3 %copy.107 = bf16[512,2048]{1,0:T(8,128)(2,1)} copy(bf16[512,2048]{0,1:T(8,128)(2,1)} %bitcast.122) | data formatting | bytes 4194304
  192.9 5.4 %fusion.13 = bf16[512,16,128]{0,2,1:T(8,128)(2,1)} fusion(f32[16,512,128]{1,2,0:T(8,128)} %fusion.8, bf16[16,128,128]{2,1,0:T(8,128)(2,1)S(1)} %add_convert_fusion, bf16[512,2048]{1,0:T(8,128)(2,1)} %param.9), kind=kOutput, calls=%fused_computation.19 | convolution fusion | flops 270532608 | bytes 8912896 | tf_op jit(solution)/shard_map/the,hde->thd/dot_general | solution.py:101
  198.4 3.9 copy.106
  202.3 11.6 %fusion.4 = f32[16,1,128,128]{3,1,2,0:T(1,128)S(1)} fusion(f32[16,16,1,1]{0,2,3,1:T(1,128)S(1)} %copy.110, bf16[16,16,128,128]{3,2,1,0:T(8,128)(2,1)} %bitcast.120), kind=kOutput, calls=%fused_computation.8 | convolution fusion | flops 50331648 | bytes 9438208 | tf_op jit(solution)/shard_map/nh,nhde->hde/dot_general | solution.py:83
  213.9 0.7 fusion.53
  214.6 14.5 %fusion.14 = bf16[512,16,128]{0,2,1:T(8,128)(2,1)} fusion(f32[16,128,512]{2,1,0:T(8,128)S(1)} %fusion.53, bf16[16,512,512]{2,0,1:T(8,128)(2,1)} %get-tuple-element.21, bf16[512,2048]{1,0:T(8,128)(2,1)S(1)} %copy-done), kind=kOutput, calls=%fused_computation.21 | convolution fusion | flops 1075838976 | bytes 16777216 | tf_op jit(solution)/shard_map/hts,shd->thd/dot_general | solution.py:53
  229.0 116.2 %reduce-scatter.2.cloned.1.call-done = f32[128,2048]{0,1:T(8,128)} async-done(((f32[2048,2048]{0,1:T(8,128)}), f32[128,2048]{0,1:T(8,128)}) %reduce-scatter.2.cloned.1.call-update) | async-done | bytes 1048592 | tf_op jit(solution)/shard_map/reduce_scatter | solution.py:110
  345.3 2.2 multiply_reduce_fusion
  347.4 4.0 copy.105
  351.4 39.5 %psum.7 = f32[]{:T(128)} all-reduce(f32[]{:T(128)} %multiply_reduce_fusion), channel_id=1, replica_groups=mesh['head'=2,'seq'=16] {'head','seq'}, use_global_device_ids=true, to_apply=%region_2.3 | all-reduce | flops 1 | bytes 8 | tf_op jit(solution)/shard_map/psum | solution.py:118
  391.6 2.3 multiply_add_fusion
  393.9 2.5 copy.108
  (25 shorter events, 0.1 us)
Async XLA Ops:
  7.2 1.6 copy-start
  7.2 195.1 %all-gather.3.cloned.1.call-start = ((), (), s32[]{:S(2)}) async-start(), calls=%async_computation.2 | async-start | bytes 8912896 | tf_op jit(solution)/shard_map/all_gather | solution.py:79
  12.1 333.2 %reduce-scatter.2.cloned.1.call-start = ((), (), s32[]{:S(2)}) async-start(), calls=%async_computation.1 | async-start | bytes 17825792 | tf_op jit(solution)/shard_map/reduce_scatter | solution.py:110
  19.1 7.3 %copy-start.10 = (s32[18,32]{1,0:T(8,128)S(1)}, s32[18,32]{1,0:T(8,128)}, u32[]{:S(2)}) copy-start(s32[18,32]{1,0:T(8,128)} %param.13) | copy-start | bytes 6916
  19.1 3.0 collective-permute-start
  19.6 6.8 %copy-start.1 = (bf16[512,2048]{0,1:T(8,128)(2,1)S(1)}, bf16[512,2048]{0,1:T(8,128)(2,1)}, u32[]{:S(2)}) copy-start(bf16[512,2048]{0,1:T(8,128)(2,1)} %copy.115) | copy-start | bytes 6291460
  23.5 33.6 %collective-permute-start.1 = (f32[16,128,128]{2,1,0:T(8,128)S(1)}, f32[16,128,128]{2,1,0:T(8,128)S(1)}, u32[]{:S(2)}, u32[]{:S(2)}) collective-permute-start(f32[16,128,128]{2,1,0:T(8,128)S(1)} %add.322), channel_id=1, source_target_pairs={{0,2},{1,3},{2,0},{3,1},{4,6},{5,7},{6,4},{7,5},{8,10},{9,11},{10,... | collective-permute-start | bytes 3145736 | tf_op jit(solution)/shard_map/ppermute | solution.py:16
  30.4 30.8 %copy-start.3 = (bf16[512,2048]{1,0:T(8,128)(2,1)S(1)}, bf16[512,2048]{1,0:T(8,128)(2,1)}, u32[]{:S(2)}) copy-start(bf16[512,2048]{1,0:T(8,128)(2,1)} %param.7) | copy-start | bytes 6291460
  57.1 4.1 %copy-start.5 = (f32[16,128,128]{2,1,0:T(8,128)}, f32[16,128,128]{2,1,0:T(8,128)S(1)}, u32[]{:S(2)}) copy-start(f32[16,128,128]{2,1,0:T(8,128)S(1)} %collective-permute-done.1) | copy-start | bytes 3145732
  57.2 49.5 %collective-permute-start.2 = (f32[16,128,128]{2,1,0:T(8,128)S(1)}, f32[16,128,128]{2,1,0:T(8,128)S(1)}, u32[]{:S(2)}, u32[]{:S(2)}) collective-permute-start(f32[16,128,128]{2,1,0:T(8,128)S(1)} %add.324), channel_id=1, source_target_pairs={{0,4},{1,5},{2,6},{3,7},{4,0},{5,1},{6,2},{7,3},{8,12},{9,13},{10,... | collective-permute-start | bytes 3145736 | tf_op jit(solution)/shard_map/ppermute | solution.py:16
  106.8 1.0 copy-start.7
  107.8 48.4 %collective-permute-start.3 = (f32[16,128,128]{2,1,0:T(8,128)S(1)}, f32[16,128,128]{2,1,0:T(8,128)}, u32[]{:S(2)}, u32[]{:S(2)}) collective-permute-start(f32[16,128,128]{2,1,0:T(8,128)S(1)} %add.326), channel_id=1, source_target_pairs={{0,8},{1,9},{2,10},{3,11},{4,12},{5,13},{6,14},{7,15},{8,0},{9,1},... | collective-permute-start | bytes 3145736 | tf_op jit(solution)/shard_map/ppermute | solution.py:16
  142.4 13.7 %copy-start.6 = (f32[16,128,128]{2,1,0:T(8,128)S(1)}, f32[16,128,128]{2,1,0:T(8,128)}, u32[]{:S(2)}) copy-start(f32[16,128,128]{2,1,0:T(8,128)} %copy-done.5) | copy-start | bytes 3145732
  142.5 13.7 %copy-start.8 = (f32[16,128,128]{2,1,0:T(8,128)S(1)}, f32[16,128,128]{2,1,0:T(8,128)}, u32[]{:S(2)}) copy-start(f32[16,128,128]{2,1,0:T(8,128)} %copy-done.7) | copy-start | bytes 3145732
  158.2 2.2 copy-start.11
  159.2 1.3 copy-start.4
  202.3 11.6 %copy-start.2 = (bf16[512,2048]{0,1:T(8,128)(2,1)S(1)}, bf16[512,2048]{0,1:T(8,128)(2,1)}, u32[]{:S(2)}) copy-start(bf16[512,2048]{0,1:T(8,128)(2,1)} %copy.115) | copy-start | bytes 6291460
  347.4 44.1 %copy-start.9 = (f32[128,2048]{0,1:T(8,128)S(1)}, f32[128,2048]{0,1:T(8,128)}, u32[]{:S(2)}) copy-start(f32[128,2048]{0,1:T(8,128)} %reduce-scatter.2.cloned.1.call-done) | copy-start | bytes 3145732
Sparse Core Ops, SparseCore 0:
  12.2 92.6 all-gather.2
  169.0 176.2 reduce-scatter.1
where the time goes:
time: 412 us; the launch traced here: 404 us
  waiting for transfers between devices  183 us (44%)
  matrix products  124 us (30%)
  blocking collectives  39.5 us (10%)
  local copies, waits for them, and re-layouts  25.1 us (6%)
  between operations  15.3 us (4%)
  other arithmetic  10.8 us (3%)
  starting transfers between devices  6.19 us (2%)
    reduce_scatter x1, waiting for transfers between devices, body(): lax.psum_scatter(lax.dot_general(inputs, value_grad, (((0,), (0,)), ((),...  116 us
    ppermute x4, waiting for transfers between devices, partner(): lax.ppermute(x, axis, [(i, i ^ 1 << apart) for i in range(lax.axis_size(a...  66.9 us
    psum x1, blocking collectives, body(): total = lax.psum(jnp.sum(shard * shard), ('head', 'seq'))  39.5 us
    dot_general x2, matrix products, lookup(): picked = jnp.dot(flat, table, precision=lax.Precision.HIGHEST)  33.8 us
    unnamed x29, local copies, waits for them, and re-layouts  21.1 us
    dot_general x1, matrix products, local_grads(): jnp.einsum('hts,thd->shd', dmix, query, preferred_element_type=jnp.float32)  16.9 us
    dot_general x1, matrix products, local_grads(): jnp.einsum('hts,shd->thd', dmix, key_rows, preferred_element_type=jnp.flo...  14.5 us
    dot_general x1, matrix products, local_grads(): jnp.einsum('hts,thd->shd', mixed, grad_rows, preferred_element_type=jnp.f...  13.2 us
  transfers between devices with their start and end apart: 6, of which 5 were waited for; matrix products, arithmetic and copies ran while one was open for 35% of the time, Pallas kernels for 0%

commit v1 on v0

v1 whole, which is shorter than its diff:
```python
import math

import jax
import jax.numpy as jnp
from jax import lax
from jax.experimental import pallas as pl
from jax.experimental.pallas import tpu as pltpu
from jax.sharding import PartitionSpec as P

D_HEAD = 128


clip_norm = 1024.0
momentum_rate = 0.9


def partner(x, axis, apart):
    return lax.ppermute(x, axis, [(i, i ^ 1 << apart) for i in range(lax.axis_size(axis))])


def sum_everywhere(x, axes):
    for axis in axes:
        for apart in range(lax.axis_size(axis).bit_length() - 1):
            x = x + partner(x, axis, apart)
    return x


def bit_length(numbers, count):
    total = jnp.zeros_like(numbers)
    for place in range(count):
        total = total + (jnp.right_shift(numbers, place) > 0).astype(jnp.int32)
    return total


def level_table(level_weight, head_size):
    levels = jnp.arange(level_weight.shape[0], dtype=jnp.float32)
    factor = jnp.exp2(-0.5 * levels) / (8.0 * math.sqrt(head_size))
    return level_weight.astype(jnp.float32) * factor[:, None]


def lookup(level, table):
    onehot = (level[..., None] == jnp.arange(table.shape[0], dtype=jnp.int32)).astype(jnp.float32)
    flat = onehot.reshape(-1, table.shape[0])
    picked = jnp.dot(flat, table, precision=lax.Precision.HIGHEST)
    return picked.reshape(level.shape + (table.shape[1],))


def dot(a, b, da, db):
    return lax.dot_general(a, b, (((da,), (db,)), ((), ())), preferred_element_type=jnp.float32)


def tile_of(length):
    return min(256, length)


def diagonal(table_ref, h, tile, key_major):
    row = lax.broadcasted_iota(jnp.int32, (tile, tile), 0)
    col = lax.broadcasted_iota(jnp.int32, (tile, tile), 1)
    apart = jnp.bitwise_xor(row, col)
    weight = jnp.full((tile, tile), table_ref[0, h], jnp.float32)
    for level in range(1, tile.bit_length()):
        weight = jnp.where(apart >= 1 << (level - 1), table_ref[level, h], weight)
    causal = row <= col if key_major else col <= row
    return jnp.where(causal, weight, jnp.float32(0.0))


def weighted(table_ref, h, diag, scores, own, first):
    tile = scores.shape[0]
    base = tile.bit_length() - 1
    parts = []
    for place in range(scores.shape[1] // tile):
        other = first + place
        block = scores[:, place * tile : (place + 1) * tile]
        if other == own:
            factor = diag
        else:
            factor = table_ref[base + (own ^ other).bit_length(), h]
        parts.append((factor * block).astype(jnp.bfloat16))
    return parts[0] if len(parts) == 1 else jnp.concatenate(parts, axis=1)


def across_sum(weight_ref, h, gathered_ref):
    total = weight_ref[0, h] * gathered_ref[0, 0].astype(jnp.float32)
    for span in range(1, gathered_ref.shape[0]):
        total = total + weight_ref[span, h] * gathered_ref[span, 0].astype(jnp.float32)
    return total.astype(jnp.bfloat16)


def sums_kernel(q_ref, k_ref, v_ref, g_ref, grads_ref, states_ref):
    states_ref[0] = dot(k_ref[...], v_ref[...], 0, 0).astype(jnp.bfloat16)
    grads_ref[0] = dot(q_ref[...], g_ref[...], 0, 0).astype(jnp.bfloat16)


def value_part_kernel(table_ref, q_ref, k_ref, g_ref, part_ref):
    h = pl.program_id(0)
    tile = tile_of(q_ref.shape[0])
    diag = diagonal(table_ref, h, tile, True)
    for j in range(q_ref.shape[0] // tile):
        rows = slice(j * tile, (j + 1) * tile)
        later = slice(j * tile, q_ref.shape[0])
        scores = dot(k_ref[rows, :], q_ref[later, :], 1, 1)
        mixed = weighted(table_ref, h, diag, scores, j, j)
        part_ref[rows, :] = dot(mixed, g_ref[later, :], 1, 0)


def value_grad_kernel(returned_ref, k_ref, part_ref, grad_ref):
    grad_ref[...] = (part_ref[...] + dot(k_ref[...], returned_ref[0], 1, 0)).astype(jnp.bfloat16)


def query_key_kernel(
    table_ref, weight_ref, gathered_ref, returned_ref, q_ref, k_ref, v_ref, g_ref, dq_ref, dk_ref
):
    h = pl.program_id(0)
    length = q_ref.shape[0]
    tile = tile_of(length)
    carried = across_sum(weight_ref, h, gathered_ref)
    returned = returned_ref[0]
    by_key = diagonal(table_ref, h, tile, True)
    by_query = diagonal(table_ref, h, tile, False)
    for i in range(length // tile):
        rows = slice(i * tile, (i + 1) * tile)
        later = slice(i * tile, length)
        upto = slice(0, (i + 1) * tile)
        before = dot(v_ref[rows, :], g_ref[later, :], 1, 1)
        dmix = weighted(table_ref, h, by_key, before, i, i)
        key_grad = dot(dmix, q_ref[later, :], 1, 0) + dot(v_ref[rows, :], returned, 1, 1)
        dk_ref[rows, :] = key_grad.astype(jnp.bfloat16)
        before = dot(g_ref[rows, :], v_ref[upto, :], 1, 1)
        dmix = weighted(table_ref, h, by_query, before, i, 0)
        query_grad = dot(dmix, k_ref[upto, :], 1, 0) + dot(g_ref[rows, :], carried, 1, 1)
        dq_ref[rows, :] = query_grad.astype(jnp.bfloat16)


def proj_kernel(x_ref, grad_ref, out_ref):
    out_ref[...] = dot(x_ref[...], grad_ref[...], 0, 0).astype(jnp.bfloat16)


def cost(flops, nbytes):
    return pl.CostEstimate(flops=flops, bytes_accessed=nbytes, transcendentals=0)


def body(queries, keys, values, out_grad, inputs, momentum, level_weight):
    length, width = queries.shape
    per_dev = width // D_HEAD
    features = inputs.shape[1]
    table_all = level_table(level_weight, D_HEAD)
    table = lax.dynamic_slice_in_dim(table_all, lax.axis_index("head") * per_dev, per_dev, 1)
    rank = lax.axis_index("seq")
    spans = lax.axis_size("seq")
    base_level = length.bit_length() - 1
    sources = jnp.arange(spans, dtype=jnp.int32)
    level = bit_length(jnp.bitwise_xor(sources, rank), table.shape[0]) + base_level
    picked = lookup(level, table)
    state_weight = jnp.where((sources < rank)[:, None], picked, jnp.float32(0.0))

    smem = pl.BlockSpec(memory_space=pltpu.SMEM)
    rows = pl.BlockSpec((length, D_HEAD), lambda h: (0, h))
    matrix = pl.BlockSpec((1, D_HEAD, D_HEAD), lambda h: (h, 0, 0))
    everyone = pl.BlockSpec((spans, 1, D_HEAD, D_HEAD), lambda h: (0, h, 0, 0))
    matrices = jax.ShapeDtypeStruct((per_dev, D_HEAD, D_HEAD), jnp.bfloat16)
    narrow = jax.ShapeDtypeStruct((length, width), jnp.bfloat16)
    wide = jax.ShapeDtypeStruct((length, width), jnp.float32)
    once = 2 * length * width
    square = 2 * length * length * width

    grads, states = pl.pallas_call(
        sums_kernel,
        grid=(per_dev,),
        in_specs=[rows, rows, rows, rows],
        out_specs=(matrix, matrix),
        out_shape=(matrices, matrices),
        cost_estimate=cost(4 * length * width * D_HEAD, 4 * once),
    )(queries, keys, values, out_grad)
    all_states = lax.all_gather(states[None], "seq", axis=0, tiled=True)
    value_part = pl.pallas_call(
        value_part_kernel,
        grid=(per_dev,),
        in_specs=[smem, rows, rows, rows],
        out_specs=rows,
        out_shape=wide,
        cost_estimate=cost(4 * square, 5 * once),
    )(table, queries, keys, out_grad)
    block = grads.astype(jnp.float32)
    grad_sum = jnp.zeros(block.shape, jnp.float32)
    for bit in range(spans.bit_length() - 1):
        other = partner(block.astype(jnp.bfloat16), "seq", bit).astype(jnp.float32)
        weight = table[base_level + bit + 1][:, None, None]
        upper = jnp.bitwise_and(jnp.right_shift(rank, bit), 1) == 1
        grad_sum = grad_sum + jnp.where(upper, jnp.float32(0.0), weight * other)
        block = block + other
    returned = grad_sum.astype(jnp.bfloat16)
    value_grad = pl.pallas_call(
        value_grad_kernel,
        grid=(per_dev,),
        in_specs=[matrix, rows, rows],
        out_specs=rows,
        out_shape=narrow,
        cost_estimate=cost(2 * length * width * D_HEAD, 4 * once),
    )(returned, keys, value_part)
    step = min(256, features)
    partial = pl.pallas_call(
        proj_kernel,
        grid=(features // step,),
        in_specs=[
            pl.BlockSpec((length, step), lambda i: (0, i)),
            pl.BlockSpec((length, width), lambda i: (0, 0)),
        ],
        out_specs=pl.BlockSpec((step, width), lambda i: (i, 0)),
        out_shape=jax.ShapeDtypeStruct((features, width), jnp.bfloat16),
        cost_estimate=cost(2 * length * width * features, 2 * features * width + 2 * once),
    )(inputs, value_grad)
    partial, all_states = lax.optimization_barrier((partial, all_states))
    shard = lax.psum_scatter(partial, "seq", scatter_dimension=0, tiled=True).astype(jnp.float32)
    query_grad, key_grad = pl.pallas_call(
        query_key_kernel,
        grid=(per_dev,),
        in_specs=[smem, smem, everyone, matrix, rows, rows, rows, rows],
        out_specs=(rows, rows),
        out_shape=(narrow, narrow),
        cost_estimate=cost(8 * square, 10 * once),
    )(table, state_weight, all_states, returned, queries, keys, values, out_grad)
    total = sum_everywhere(jnp.sum(shard * shard), ("head", "seq"))
    factor = jnp.minimum(jnp.float32(1.0), clip_norm / jnp.sqrt(total + 1e-06))
    new_momentum = momentum_rate * momentum + factor * shard
    return (query_grad, key_grad, value_grad, new_momentum)


def solution(mesh):
    placed = (
        P("seq", "head"),
        P("seq", "head"),
        P("seq", "head"),
        P("seq", "head"),
        P("seq", None),
        P("seq", "head"),
        P(),
    )
    return jax.shard_map(
        body,
        mesh=mesh,
        in_specs=placed,
        out_specs=(P("seq", "head"), P("seq", "head"), P("seq", "head"), P("seq", "head")),
        check_vma=False,
    )
```

time: 412 us -> 278 us (0.67); the launches traced: 404 us -> 276 us
  matrix products: 124 us -> 0.79 us
  Pallas kernels: 0 us -> 69 us
  blocking collectives: 39.5 us -> 0 us
  local copies, waits for them, and re-layouts: 25.1 us -> 0.66 us
  waiting for transfers between devices: 183 us -> 161 us
  starting transfers between devices: 6.19 us -> 19.4 us
    dot_general x12 -> x0, matrix products: 89.9 us -> none  [the longest x1 16.9 us: local_grads(): jnp.einsum('hts,thd->shd', dmix, query, preferred_element_type=jnp.float32)]
    pallas_call x0 -> x5, Pallas kernels: none -> 69 us  [the longest x1 19.6 us: body(): pl.pallas_call(query_key_kernel, grid=(per_dev,), in_specs=[smem, smem, e...]
    psum x1 -> x0, blocking collectives: 39.5 us -> none  [body(): total = lax.psum(jnp.sum(shard * shard), ('head', 'seq'))]
    reduce_scatter x1, waiting for transfers between devices: 116 us -> 82.6 us  [body(): lax.psum_scatter(partial, 'seq', scatter_dimension=0, tiled=True)]
    dot_general x2 -> x1, matrix products: 33.8 us -> 0.79 us  [lookup(): picked = jnp.dot(flat, table, precision=lax.Precision.HIGHEST)]
    unnamed x29 -> x10, local copies, waits for them, and re-layouts: 21.1 us -> 0.66 us
    ppermute x4 -> x9, starting transfers between devices: 6.11 us -> 19.4 us  [partner(): lax.ppermute(x, axis, [(i, i ^ 1 << apart) for i in range(lax.axis_size(a...]
    ppermute x4 -> x9, waiting for transfers between devices: 66.9 us -> 78.2 us  [partner(): lax.ppermute(x, axis, [(i, i ^ 1 << apart) for i in range(lax.axis_size(a...]
  transfers between devices with their start and end apart: 6 -> 11, of which waited for: 5 -> 10; matrix products, arithmetic and copies ran while one was open for 35% -> 1% of each run, Pallas kernels for 0% -> 21%
where the time goes in v1:
time: 278 us; the launch traced here: 276 us
  waiting for transfers between devices  161 us (58%)
  Pallas kernels  69 us (25%)
  starting transfers between devices  19.4 us (7%)
  between operations  17.5 us (6%)
  other arithmetic  7.41 us (3%)
    reduce_scatter x1, waiting for transfers between devices, body(): lax.psum_scatter(partial, 'seq', scatter_dimension=0, tiled=True)  82.6 us
    ppermute x9, waiting for transfers between devices, partner(): lax.ppermute(x, axis, [(i, i ^ 1 << apart) for i in range(lax.axis_size(a...  78.2 us
    pallas_call x1, Pallas kernels, body(): pl.pallas_call(query_key_kernel, grid=(per_dev,), in_specs=[smem, smem, e...  19.6 us
    ppermute x9, starting transfers between devices, partner(): lax.ppermute(x, axis, [(i, i ^ 1 << apart) for i in range(lax.axis_size(a...  19.4 us
    pallas_call x1, Pallas kernels, body(): pl.pallas_call(value_part_kernel, grid=(per_dev,), in_specs=[smem, rows,...  15.1 us
    pallas_call x1, Pallas kernels, body(): pl.pallas_call(sums_kernel, grid=(per_dev,), in_specs=[rows, rows, rows,...  12.2 us
    pallas_call x1, Pallas kernels, body(): pl.pallas_call(value_grad_kernel, grid=(per_dev,), in_specs=[matrix, rows...  12 us
    pallas_call x1, Pallas kernels, body(): pl.pallas_call(proj_kernel, grid=(features // step,), in_specs=[pl.BlockS...  10.1 us
  transfers between devices with their start and end apart: 11, of which 10 were waited for; matrix products, arithmetic and copies ran while one was open for 1% of the time, Pallas kernels for 21%

profile of v1, /device:TPU:0, one launch (start us, length us, event | category | flops | bytes accessed | tf_op | source)
XLA Modules:
  0.0 275.7 jit_solution(10988765492603851798)
XLA Ops:
  7.2 0.0 all-gather.3.cloned.1.call-start
  7.2 12.2 %shard_map.102 = (bf16[16,128,128]{2,1,0:T(8,128)(2,1)}, bf16[16,128,128]{2,1,0:T(8,128)(2,1)}) custom-call(bf16[512,2048]{1,0:T(8,128)(2,1)} %q_ref.5, bf16[512,2048]{1,0:T(8,128)(2,1)} %k_ref.7, bf16[512,2048]{1,0:T(8,128)(2,1)} %v_ref.3, bf16[512,2048]{1,0:T(8,128)(2,1)} %g_ref.5), custom_call_target="tpu_custom_call" | custom-call | flops 536870912 | bytes 8388608 | tf_op jit(solution)/shard_map/pallas_call | solution.py:166
  19.4 0.0 copy-start
  19.4 0.0 copy-start.4
  19.5 0.0 all-gather.3.cloned.1.call-update
  19.5 0.0 reduce-scatter.2.cloned.1.call-start
  19.5 0.6 collective-permute-start
  20.1 1.7 collective-permute-done
  21.8 1.2 fusion.10
  23.0 2.9 %collective-permute-start.1 = (bf16[16,128,128]{2,1,0:T(8,128)(2,1)S(1)}, bf16[16,128,128]{2,1,0:T(8,128)(2,1)S(1)}, u32[]{:S(2)}, u32[]{:S(2)}) collective-permute-start(bf16[16,128,128]{2,1,0:T(8,128)(2,1)S(1)} %fusion.10), channel_id=1, source_target_pairs={{0,2},{1,3},{2,0},{3,1},{4,6},{5,7},{6,4},{7,5},{8,10},{9,11},{10,... | collective-permute-start | bytes 1572872 | tf_op jit(solution)/shard_map/ppermute | solution.py:18
  26.0 17.8 %collective-permute-done.1 = bf16[16,128,128]{2,1,0:T(8,128)(2,1)S(1)} collective-permute-done((bf16[16,128,128]{2,1,0:T(8,128)(2,1)S(1)}, bf16[16,128,128]{2,1,0:T(8,128)(2,1)S(1)}, u32[]{:S(2)}, u32[]{:S(2)}) %collective-permute-start.1) | collective-permute-done | bytes 524320 | tf_op jit(solution)/shard_map/ppermute | solution.py:18
  43.8 0.0 copy-done
  43.8 0.2 fusion.11
  44.0 1.9 collective-permute-start.2
  45.9 0.0 copy-done.4
  45.9 0.1 fusion.12.table_ref
  46.0 0.0 copy-start.2
  46.0 18.3 %collective-permute-done.2 = bf16[16,128,128]{2,1,0:T(8,128)(2,1)S(1)} collective-permute-done((bf16[16,128,128]{2,1,0:T(8,128)(2,1)S(1)}, bf16[16,128,128]{2,1,0:T(8,128)(2,1)S(1)}, u32[]{:S(2)}, u32[]{:S(2)}) %collective-permute-start.2) | collective-permute-done | bytes 524320 | tf_op jit(solution)/shard_map/ppermute | solution.py:18
  64.3 0.4 fusion.7
  64.7 2.1 collective-permute-start.3
  66.8 0.0 copy-done.2
  66.8 15.1 %shard_map.103.part_ref = f32[512,2048]{1,0:T(8,128)} custom-call(f32[18,16]{1,0:T(8,128)} %copy-done.2, bf16[512,2048]{1,0:T(8,128)(2,1)} %q_ref.5, bf16[512,2048]{1,0:T(8,128)(2,1)} %k_ref.7, bf16[512,2048]{1,0:T(8,128)(2,1)} %g_ref.5), custom_call_target="tpu_custom_call" | custom-call | flops 4294967296 | bytes 10485760 | tf_op jit(solution)/shard_map/pallas_call | solution.py:175
  81.9 34.9 %collective-permute-done.3 = bf16[16,128,128]{2,1,0:T(8,128)(2,1)S(1)} collective-permute-done((bf16[16,128,128]{2,1,0:T(8,128)(2,1)S(1)}, bf16[16,128,128]{2,1,0:T(8,128)(2,1)S(1)}, u32[]{:S(2)}, u32[]{:S(2)}) %collective-permute-start.3) | collective-permute-done | bytes 524320 | tf_op jit(solution)/shard_map/ppermute | solution.py:18
  116.8 1.4 fusion.4.returned_ref
  118.2 12.0 %shard_map.104.grad_ref = bf16[512,2048]{1,0:T(8,128)(2,1)} custom-call(bf16[16,128,128]{2,1,0:T(8,128)(2,1)} %fusion.4.returned_ref, bf16[512,2048]{1,0:T(8,128)(2,1)} %k_ref.7, f32[512,2048]{1,0:T(8,128)} %shard_map.103.part_ref), custom_call_target="tpu_custom_call" | custom-call | flops 268435456 | bytes 8388608 | tf_op jit(solution)/shard_map/pallas_call | solution.py:192
  130.2 10.1 %shard_map.105 = bf16[2048,2048]{1,0:T(8,128)(2,1)} custom-call(bf16[512,2048]{1,0:T(8,128)(2,1)} %x_ref.1, bf16[512,2048]{1,0:T(8,128)(2,1)} %shard_map.104.grad_ref), custom_call_target="tpu_custom_call" | custom-call | flops 4294967296 | bytes 12582912 | tf_op jit(solution)/shard_map/pallas_call | solution.py:201
  140.3 0.0 all-gather.3.cloned.1.call-done
  140.3 0.0 copy-start.3
  140.3 0.0 reduce-scatter.2.cloned.1.call-update
  140.4 0.6 copy-done.3
  141.0 0.8 convolution_select_fusion.weight_ref
  141.8 0.0 copy-start.1
  141.8 19.6 %shard_map.106 = (bf16[512,2048]{1,0:T(8,128)(2,1)}, bf16[512,2048]{1,0:T(8,128)(2,1)}) custom-call(f32[18,16]{1,0:T(8,128)} %copy-done.2, f32[16,16]{1,0:T(8,128)} %convolution_select_fusion.weight_ref, bf16[16,16,128,128]{3,2,1,0:T(8,128)(2,1)} %bitcast.10, bf16[16,128,128]{2,1,0:T(8,128)(2,1)} %fusion.4.returned_ref, bf16[512,2048]{1,0:T(8,128)(2,1)} %q_ref.5, ...), custom_call_target="tpu_custom_call" | custom-call | flops 8589934592 | bytes 20971520 | tf_op jit(solution)/shard_map/pallas_call | solution.py:214
  161.4 82.6 %reduce-scatter.2.cloned.1.call-done = bf16[128,2048]{1,0:T(8,128)(2,1)} async-done(((bf16[2048,2048]{1,0:T(8,128)(2,1)}), bf16[128,2048]{1,0:T(8,128)(2,1)}) %reduce-scatter.2.cloned.1.call-update) | async-done | bytes 524304 | tf_op jit(solution)/shard_map/reduce_scatter | solution.py:213
  244.0 1.9 fusion.8
  245.9 1.5 collective-permute-start.4
  247.4 2.3 collective-permute-done.4
  250.9 1.0 collective-permute-start.5
  252.0 0.3 collective-permute-done.5
  252.9 2.8 %collective-permute-start.6 = (f32[]{:T(128)}, f32[]{:T(128)}, u32[]{:S(2)}, u32[]{:S(2)}) collective-permute-start(f32[]{:T(128)} %add.196), channel_id=1, source_target_pairs={{0,2},{1,3},{2,0},{3,1},{4,6},{5,7},{6,4},{7,5},{8,10},{9,11},{10,... | collective-permute-start | bytes 20 | tf_op jit(solution)/shard_map/ppermute | solution.py:18
  255.7 0.9 collective-permute-done.6
  257.1 3.1 %collective-permute-start.7 = (f32[]{:T(128)}, f32[]{:T(128)}, u32[]{:S(2)}, u32[]{:S(2)}) collective-permute-start(f32[]{:T(128)} %add.197), channel_id=1, source_target_pairs={{0,4},{1,5},{2,6},{3,7},{4,0},{5,1},{6,2},{7,3},{8,12},{9,13},{10,... | collective-permute-start | bytes 20 | tf_op jit(solution)/shard_map/ppermute | solution.py:18
  260.2 0.7 collective-permute-done.7
  261.4 3.4 %collective-permute-start.8 = (f32[]{:T(128)}, f32[]{:T(128)}, u32[]{:S(2)}, u32[]{:S(2)}) collective-permute-start(f32[]{:T(128)} %add.198), channel_id=1, source_target_pairs={{0,8},{1,9},{2,10},{3,11},{4,12},{5,13},{6,14},{7,15},{8,0},{9,1},... | collective-permute-start | bytes 20 | tf_op jit(solution)/shard_map/ppermute | solution.py:18
  264.9 1.2 collective-permute-done.8
  266.7 0.0 copy-done.1
  266.7 2.2 fusion.9
  (4 shorter events, 0.0 us)
Async XLA Ops:
  7.2 133.2 %all-gather.3.cloned.1.call-start = ((), (), s32[]{:S(2)}) async-start(), calls=%async_computation.2 | async-start | bytes 8912896 | tf_op jit(solution)/shard_map/all_gather | solution.py:174
  19.4 24.3 %copy-start = (bf16[16,128,128]{2,1,0:T(8,128)(2,1)S(1)}, bf16[16,128,128]{2,1,0:T(8,128)(2,1)}, u32[]{:S(2)}) copy-start(bf16[16,128,128]{2,1,0:T(8,128)(2,1)} %get-tuple-element.10) | copy-start | bytes 1572868
  19.4 26.5 %copy-start.4 = (s32[18,32]{1,0:T(8,128)S(1)}, s32[18,32]{1,0:T(8,128)}, u32[]{:S(2)}) copy-start(s32[18,32]{1,0:T(8,128)} %param.13) | copy-start | bytes 6916
  19.5 224.5 %reduce-scatter.2.cloned.1.call-start = ((), (), s32[]{:S(2)}) async-start(), calls=%async_computation.1 | async-start | bytes 8912896 | tf_op jit(solution)/shard_map/reduce_scatter | solution.py:213
  19.5 2.3 collective-permute-start
  23.0 20.7 %collective-permute-start.1 = (bf16[16,128,128]{2,1,0:T(8,128)(2,1)S(1)}, bf16[16,128,128]{2,1,0:T(8,128)(2,1)S(1)}, u32[]{:S(2)}, u32[]{:S(2)}) collective-permute-start(bf16[16,128,128]{2,1,0:T(8,128)(2,1)S(1)} %fusion.10), channel_id=1, source_target_pairs={{0,2},{1,3},{2,0},{3,1},{4,6},{5,7},{6,4},{7,5},{8,10},{9,11},{10,... | collective-permute-start | bytes 1572872 | tf_op jit(solution)/shard_map/ppermute | solution.py:18
  44.0 20.3 %collective-permute-start.2 = (bf16[16,128,128]{2,1,0:T(8,128)(2,1)S(1)}, bf16[16,128,128]{2,1,0:T(8,128)(2,1)S(1)}, u32[]{:S(2)}, u32[]{:S(2)}) collective-permute-start(bf16[16,128,128]{2,1,0:T(8,128)(2,1)S(1)} %fusion.11), channel_id=1, source_target_pairs={{0,4},{1,5},{2,6},{3,7},{4,0},{5,1},{6,2},{7,3},{8,12},{9,13},{10,... | collective-permute-start | bytes 1572872 | tf_op jit(solution)/shard_map/ppermute | solution.py:18
  46.0 20.8 %copy-start.2 = (f32[18,16]{1,0:T(8,128)}, f32[18,16]{1,0:T(8,128)S(1)}, u32[]{:S(2)}) copy-start(f32[18,16]{1,0:T(8,128)S(1)} %fusion.12.table_ref) | copy-start | bytes 3460
  64.7 52.1 %collective-permute-start.3 = (bf16[16,128,128]{2,1,0:T(8,128)(2,1)S(1)}, bf16[16,128,128]{2,1,0:T(8,128)(2,1)S(1)}, u32[]{:S(2)}, u32[]{:S(2)}) collective-permute-start(bf16[16,128,128]{2,1,0:T(8,128)(2,1)S(1)} %fusion.7), channel_id=1, source_target_pairs={{0,8},{1,9},{2,10},{3,11},{4,12},{5,13},{6,14},{7,15},{8,0},{9,1},... | collective-permute-start | bytes 1572872 | tf_op jit(solution)/shard_map/ppermute | solution.py:18
  140.3 0.7 copy-start.3
  141.8 124.8 %copy-start.1 = (f32[128,2048]{1,0:T(8,128)S(1)}, f32[128,2048]{1,0:T(8,128)}, u32[]{:S(2)}) copy-start(f32[128,2048]{1,0:T(8,128)} %param.12) | copy-start | bytes 3145732
  245.9 3.8 %collective-permute-start.4 = (f32[]{:T(128)}, f32[]{:T(128)}, u32[]{:S(2)}, u32[]{:S(2)}) collective-permute-start(f32[]{:T(128)} %fusion.8), channel_id=1, source_target_pairs={{0,16},{16,0},{1,17},{17,1},{2,18},{18,2},{3,19},{19,3},{4,20},{20... | collective-permute-start | bytes 20 | tf_op jit(solution)/shard_map/ppermute | solution.py:18
  250.9 1.4 collective-permute-start.5
  252.9 3.7 %collective-permute-start.6 = (f32[]{:T(128)}, f32[]{:T(128)}, u32[]{:S(2)}, u32[]{:S(2)}) collective-permute-start(f32[]{:T(128)} %add.196), channel_id=1, source_target_pairs={{0,2},{1,3},{2,0},{3,1},{4,6},{5,7},{6,4},{7,5},{8,10},{9,11},{10,... | collective-permute-start | bytes 20 | tf_op jit(solution)/shard_map/ppermute | solution.py:18
  257.1 3.7 %collective-permute-start.7 = (f32[]{:T(128)}, f32[]{:T(128)}, u32[]{:S(2)}, u32[]{:S(2)}) collective-permute-start(f32[]{:T(128)} %add.197), channel_id=1, source_target_pairs={{0,4},{1,5},{2,6},{3,7},{4,0},{5,1},{6,2},{7,3},{8,12},{9,13},{10,... | collective-permute-start | bytes 20 | tf_op jit(solution)/shard_map/ppermute | solution.py:18
  261.4 4.6 %collective-permute-start.8 = (f32[]{:T(128)}, f32[]{:T(128)}, u32[]{:S(2)}, u32[]{:S(2)}) collective-permute-start(f32[]{:T(128)} %add.198), channel_id=1, source_target_pairs={{0,8},{1,9},{2,10},{3,11},{4,12},{5,13},{6,14},{7,15},{8,0},{9,1},... | collective-permute-start | bytes 20 | tf_op jit(solution)/shard_map/ppermute | solution.py:18
Sparse Core Ops, SparseCore 0:
  19.6 106.1 all-gather.2
  140.5 103.4 reduce-scatter.1
